TPU v7x, 32 devices: a whole 2x2x4 slice. The times are simulated.
32 devices in a mesh: rows: 8 (over z, x), head: 4 (over y, core).
Axes of the slice: x: 2, y: 2, z: 4, core: 2. Of those that a mesh axis runs over, the one named last changes fastest.
Arguments:
- inputs: bfloat16 [2, 32, 512, 768], P(None, ('rows', 'head')), may hold values from -6 to 6
- qkv_weight: bfloat16 [768, 2304], P('rows', 'head'), may hold values from -0.3125 to 0.3125
- out_weight: bfloat16 [768, 768], P('rows', 'head'), may hold values from -0.625 to 0.625
- up_weight: bfloat16 [768, 3072], P('rows', 'head'), may hold values from -0.21875 to 0.21875
- down_weight: bfloat16 [3072, 768], P('rows', 'head'), may hold values from -0.109375 to 0.109375
- biases: bfloat16 [8, 768], P('head', 'rows'), may hold values from -1.1953125 to 1.1953125
- norm_params: bfloat16 [4, 768], P('head', 'rows'), may hold values from -0.6 to 1.65
- cotangent: bfloat16 [2, 32, 512, 768], P(None, ('rows', 'head')), may hold values from -6 to 6
- boundaries: int32 [2, 32], P(None, 'rows'), may hold values from 1 to 511, as said below
- lengths: int32 [2, 32], P(None, 'rows'), may hold values from 257 to 512, as said below
Outputs:
- output: bfloat16 [2, 32, 512, 768], P(None, ('rows', 'head'))
- input_grad: float32 [2, 32, 512, 768], P(None, ('rows', 'head'))
- qkv_grad: float32 [768, 2304], P('rows', 'head')
- out_grad: float32 [768, 768], P('rows', 'head')
- up_grad: float32 [768, 3072], P('rows', 'head')
- down_grad: float32 [3072, 768], P('rows', 'head')
- bias_grad: float32 [8, 768], P('head', 'rows')
- norm_grad: float32 [4, 768], P('head', 'rows')
Inputs may be any that keep to these rules, and one draw needn't show every extreme that they name: `boundaries`: each row's boundary lies below its own length, so both sentences of a row hold tokens. `lengths`: every length exceeds half of 512.
All inputs are finite; a program needn't handle non-finite values.
Results may differ from a plain program's by a relative error of at most 0.017.
The roundings to bfloat16 on the way count: a program that leaves them out, or rounds other values in their place, can miss the bound.
Values may be sent and summed in bfloat16 or wider, within the bound.
A program may use at most 192 MiB of HBM per device.

v0:
```python
import jax
import jax.numpy as jnp
from jax import lax
from jax.sharding import PartitionSpec as P

D = 768
HEADS = 12
HD = 64
FF = 3072
SEQ = 512
EPSILON = 1e-06
ROOT_HALF = 0.7071067811865476
INVERSE_ROOT_TWO_PI = 0.3989422804014327


def contract_rows(left, right):
    return lax.dot_general(
        left, right, (((0,), (0,)), ((), ())), preferred_element_type=jnp.float32
    )


def contract_cols(left, right):
    return lax.dot_general(
        left, right, (((1,), (1,)), ((), ())), preferred_element_type=jnp.float32
    )


def norm_forward(values_in, gain_row, shift_row):
    average = jnp.mean(values_in, axis=-1, keepdims=True)
    centered = values_in - average
    variance = jnp.mean(centered * centered, axis=-1, keepdims=True)
    inverse_scale = lax.rsqrt(variance + EPSILON)
    normed = centered * inverse_scale
    return (normed * gain_row + shift_row, normed, inverse_scale)


def norm_backward(grad_out, normed, inverse_scale, gain_row):
    grad_normed = grad_out * gain_row
    first_mean = jnp.mean(grad_normed, axis=-1, keepdims=True)
    second_mean = jnp.mean(grad_normed * normed, axis=-1, keepdims=True)
    grad_in = inverse_scale * (grad_normed - first_mean - normed * second_mean)
    return (grad_in, jnp.sum(grad_out * normed, axis=0), jnp.sum(grad_out, axis=0))


def masked_scores(queries, keys_in, bound, length):
    positions = lax.broadcasted_iota(jnp.int32, (SEQ,), 0)
    segment = positions >= bound
    allowed = (segment[:, None] == segment[None, :]) & (positions[None, :] < length)
    scores = jnp.einsum(
        "qhe,khe->hqk", queries, keys_in, preferred_element_type=jnp.float32
    ) * HD ** (-0.5)
    return jnp.where(allowed[None], scores, -1e30)


def attend_forward(pieces):
    queries, keys_in, values_in, bound, length = pieces
    scores = masked_scores(queries, keys_in, bound, length)
    highest = jnp.max(scores, axis=-1, keepdims=True)
    raised = jnp.exp(scores - highest)
    totals = jnp.sum(raised, axis=-1, keepdims=True)
    weights_low = (raised / totals).astype(jnp.bfloat16)
    context = jnp.einsum("hqk,khe->qhe", weights_low, values_in, preferred_element_type=jnp.float32)
    log_total = (highest + jnp.log(totals))[..., 0]
    return (context.astype(jnp.bfloat16), log_total)


def attend_backward(pieces):
    queries, keys_in, values_in, bound, length, log_total, grad_context = pieces
    scores = masked_scores(queries, keys_in, bound, length)
    weights_full = jnp.exp(scores - log_total[..., None])
    weights_low = weights_full.astype(jnp.bfloat16)
    grad_values = jnp.einsum(
        "hqk,qhe->khe", weights_low, grad_context, preferred_element_type=jnp.float32
    )
    grad_weights = jnp.einsum(
        "qhe,khe->hqk", grad_context, values_in, preferred_element_type=jnp.float32
    )
    inner_sum = jnp.sum(weights_full * grad_weights, axis=-1, keepdims=True)
    grad_scores = (weights_full * (grad_weights - inner_sum)).astype(jnp.bfloat16)
    grad_queries = jnp.einsum(
        "hqk,khe->qhe", grad_scores, keys_in, preferred_element_type=jnp.float32
    ) * HD ** (-0.5)
    grad_keys = jnp.einsum(
        "hqk,qhe->khe", grad_scores, queries, preferred_element_type=jnp.float32
    ) * HD ** (-0.5)
    return jnp.stack([grad_queries, grad_keys, grad_values], axis=2).astype(jnp.bfloat16)


def split_heads(project, bounds, lengths_here, groups):
    seq_per = project.shape[0] // SEQ
    heads_dev = HEADS // groups
    spread = project.reshape(seq_per, SEQ, groups, 3 * D // groups)
    items = lax.all_to_all(spread, "head", split_axis=2, concat_axis=0, tiled=True)
    return (items.reshape(-1, SEQ, heads_dev, 3, HD), bounds, lengths_here)


def merge_heads(context_items, seq_per):
    width = context_items.shape[2] * HD
    joined = lax.all_to_all(
        context_items.reshape(-1, SEQ, 1, width), "head", split_axis=0, concat_axis=2, tiled=True
    )
    return joined.reshape(seq_per * SEQ, D)


def grad_to_items(grad_context, seq_per, groups):
    heads_dev = HEADS // groups
    spread = grad_context.reshape(seq_per, SEQ, groups, D // groups)
    items = lax.all_to_all(spread, "head", split_axis=2, concat_axis=0, tiled=True)
    return items.reshape(-1, SEQ, heads_dev, HD)


def grad_to_tokens(grad_items, seq_per):
    width = grad_items.shape[2] * 3 * HD
    joined = lax.all_to_all(
        grad_items.reshape(-1, SEQ, 1, width), "head", split_axis=0, concat_axis=2, tiled=True
    )
    return joined.reshape(seq_per * SEQ, 3 * D)


def gather_weights(qkv_weight, out_weight, up_weight, down_weight, biases, norm_params):
    by_head = (
        lax.all_gather(qkv_weight, "head", axis=1, tiled=True),
        lax.all_gather(out_weight, "head", axis=1, tiled=True),
        lax.all_gather(up_weight, "head", axis=1, tiled=True),
        lax.all_gather(down_weight, "head", axis=1, tiled=True),
        lax.all_gather(biases, "head", axis=0, tiled=True),
        lax.all_gather(norm_params, "head", axis=0, tiled=True),
    )
    return (
        lax.all_gather(by_head[0], "rows", axis=0, tiled=True),
        lax.all_gather(by_head[1], "rows", axis=0, tiled=True),
        lax.all_gather(by_head[2], "rows", axis=0, tiled=True),
        lax.all_gather(by_head[3], "rows", axis=0, tiled=True),
        lax.all_gather(by_head[4], "rows", axis=1, tiled=True),
        lax.all_gather(by_head[5], "rows", axis=1, tiled=True),
    )


def reduce_grads(running):
    rows_done = (
        lax.psum_scatter(running[0], "rows", scatter_dimension=0, tiled=True),
        lax.psum_scatter(running[1], "rows", scatter_dimension=0, tiled=True),
        lax.psum_scatter(running[2], "rows", scatter_dimension=0, tiled=True),
        lax.psum_scatter(running[3], "rows", scatter_dimension=0, tiled=True),
        lax.psum_scatter(running[4], "rows", scatter_dimension=1, tiled=True),
        lax.psum_scatter(running[5], "rows", scatter_dimension=1, tiled=True),
    )
    return (
        lax.psum_scatter(
            rows_done[0].astype(jnp.bfloat16), "head", scatter_dimension=1, tiled=True
        ).astype(jnp.float32),
        lax.psum_scatter(
            rows_done[1].astype(jnp.bfloat16), "head", scatter_dimension=1, tiled=True
        ).astype(jnp.float32),
        lax.psum_scatter(
            rows_done[2].astype(jnp.bfloat16), "head", scatter_dimension=1, tiled=True
        ).astype(jnp.float32),
        lax.psum_scatter(
            rows_done[3].astype(jnp.bfloat16), "head", scatter_dimension=1, tiled=True
        ).astype(jnp.float32),
        lax.psum_scatter(
            rows_done[4].astype(jnp.bfloat16), "head", scatter_dimension=0, tiled=True
        ).astype(jnp.float32),
        lax.psum_scatter(
            rows_done[5].astype(jnp.bfloat16), "head", scatter_dimension=0, tiled=True
        ).astype(jnp.float32),
    )


def layer_step(params, block_in, block_cot, bounds, lengths_here):
    qkv_full, out_full, up_full, down_full, bias_full, norm_full = params
    seq_per = block_in.shape[0]
    groups = lax.axis_size("head")
    tokens = block_in.reshape(seq_per * SEQ, D)
    bias_float = bias_full.astype(jnp.float32)
    norm_float = norm_full.astype(jnp.float32)
    zero_part = jnp.zeros((HEADS, HD), jnp.float32)
    head_bias = jnp.stack(
        [bias_float[0].reshape(HEADS, HD), zero_part, bias_float[1].reshape(HEADS, HD)], axis=1
    ).reshape(3 * D)
    project = (jnp.dot(tokens, qkv_full, preferred_element_type=jnp.float32) + head_bias).astype(
        jnp.bfloat16
    )
    items, item_bounds, item_lengths = split_heads(project, bounds, lengths_here, groups)
    queries = items[:, :, :, 0]
    keys_all = items[:, :, :, 1]
    values_all = items[:, :, :, 2]
    context_items, log_total = lax.map(
        attend_forward, (queries, keys_all, values_all, item_bounds, item_lengths)
    )
    context_tok = merge_heads(context_items, seq_per)
    attended = jnp.dot(context_tok, out_full, preferred_element_type=jnp.float32) + bias_float[2]
    hidden, normed_one, scale_one = norm_forward(
        tokens.astype(jnp.float32) + attended, norm_float[0], norm_float[1]
    )
    hidden_low = hidden.astype(jnp.bfloat16)
    inner_pre = jnp.dot(hidden_low, up_full, preferred_element_type=jnp.float32) + bias_float[
        4:8
    ].reshape(FF)
    active_low = jax.nn.gelu(inner_pre, approximate=False).astype(jnp.bfloat16)
    outer_out = jnp.dot(active_low, down_full, preferred_element_type=jnp.float32) + bias_float[3]
    output_float, normed_two, scale_two = norm_forward(
        hidden + outer_out, norm_float[2], norm_float[3]
    )
    output_block = output_float.astype(jnp.bfloat16).reshape(seq_per, SEQ, D)
    grad_out = block_cot.reshape(seq_per * SEQ, D).astype(jnp.float32)
    grad_two, gain_two, shift_two = norm_backward(grad_out, normed_two, scale_two, norm_float[2])
    grad_two_low = grad_two.astype(jnp.bfloat16)
    down_grad = contract_rows(active_low, grad_two_low)
    grad_active = contract_cols(grad_two_low, down_full)
    slope = (
        0.5 * (1.0 + lax.erf(inner_pre * ROOT_HALF))
        + inner_pre * jnp.exp(-0.5 * inner_pre * inner_pre) * INVERSE_ROOT_TWO_PI
    )
    grad_inner = grad_active * slope
    grad_inner_low = grad_inner.astype(jnp.bfloat16)
    up_grad = contract_rows(hidden_low, grad_inner_low)
    grad_hidden = contract_cols(grad_inner_low, up_full) + grad_two
    grad_one, gain_one, shift_one = norm_backward(grad_hidden, normed_one, scale_one, norm_float[0])
    grad_one_low = grad_one.astype(jnp.bfloat16)
    out_grad = contract_rows(context_tok, grad_one_low)
    grad_context = contract_cols(grad_one_low, out_full).astype(jnp.bfloat16)
    grad_items = grad_to_items(grad_context, seq_per, groups)
    grad_project_items = lax.map(
        attend_backward,
        (queries, keys_all, values_all, item_bounds, item_lengths, log_total, grad_items),
    )
    grad_project = grad_to_tokens(grad_project_items, seq_per)
    qkv_grad = contract_rows(tokens, grad_project)
    grad_input = contract_cols(grad_project, qkv_full) + grad_one
    project_sums = jnp.sum(grad_project, axis=0, dtype=jnp.float32).reshape(HEADS, 3, HD)
    bias_grad = jnp.concatenate(
        [
            project_sums[:, 0].reshape(1, D),
            project_sums[:, 2].reshape(1, D),
            jnp.sum(grad_one, axis=0).reshape(1, D),
            jnp.sum(grad_two, axis=0).reshape(1, D),
            jnp.sum(grad_inner, axis=0).reshape(4, D),
        ],
        axis=0,
    )
    norm_grad = jnp.stack([gain_one, shift_one, gain_two, shift_two])
    return (
        output_block,
        grad_input.reshape(seq_per, SEQ, D),
        (qkv_grad, out_grad, up_grad, down_grad, bias_grad, norm_grad),
    )


def shards(
    inputs,
    qkv_weight,
    out_weight,
    up_weight,
    down_weight,
    biases,
    norm_params,
    cotangent,
    boundaries,
    lengths,
):
    outputs_all = []
    inputs_grads = []
    running = None
    for micro_index in range(inputs.shape[0]):
        params = gather_weights(qkv_weight, out_weight, up_weight, down_weight, biases, norm_params)
        output_block, grad_block, grads_now = layer_step(
            params,
            inputs[micro_index],
            cotangent[micro_index],
            boundaries[micro_index],
            lengths[micro_index],
        )
        outputs_all.append(output_block)
        inputs_grads.append(grad_block)
        if micro_index == 0:
            running = grads_now
        else:
            running = tuple((sum_now + add_now for sum_now, add_now in zip(running, grads_now)))
    final = reduce_grads(running)
    return (
        jnp.stack(outputs_all),
        jnp.stack(inputs_grads),
        final[0],
        final[1],
        final[2],
        final[3],
        final[4],
        final[5],
    )


def solution(mesh):
    placed = (
        P(None, ("rows", "head"), None, None),
        P("rows", "head"),
        P("rows", "head"),
        P("rows", "head"),
        P("rows", "head"),
        P("head", "rows"),
        P("head", "rows"),
        P(None, ("rows", "head"), None, None),
        P(None, "rows"),
        P(None, "rows"),
    )
    return jax.shard_map(
        shards,
        mesh=mesh,
        in_specs=placed,
        out_specs=(
            P(None, ("rows", "head"), None, None),
            P(None, ("rows", "head"), None, None),
            P("rows", "head"),
            P("rows", "head"),
            P("rows", "head"),
            P("rows", "head"),
            P("head", "rows"),
            P("head", "rows"),
        ),
        check_vma=False,
    )
```

profile of v0, /device:TPU:0, one launch (start us, length us, event | category | flops | bytes accessed | tf_op | source)
XLA Modules:
  0.0 1183.9 jit_solution(4016477285375403573)
XLA Ops:
  7.2 8.8 all-gather
  38.1 27.4 %all-gather.2 = bf16[8,96,8]{1,2,0:T(8,128)(2,1)S(1)} all-gather(bf16[1,96,8]{1,2,0:T(8,128)(2,1)S(1)} %bitcast.451), channel_id=1, replica_groups=mesh['rows'=8,'head'=4] {'rows'}, dimensions={0}, use_global_device_ids=true | all-gather | bytes 13824 | tf_op jit(solution)/shard_map/all_gather | solution.py:134
  66.6 16.7 %all-gather.10.cloned.1.call-done = bf16[768,2304]{1,0:T(8,128)(2,1)} async-done(((bf16[96,2304]{1,0:T(8,128)(2,1)}), bf16[768,2304]{1,0:T(8,128)(2,1)}) %all-gather.10.cloned.1.call-update) | async-done | bytes 3538960 | tf_op jit(solution)/shard_map/all_gather | solution.py:130
  93.9 32.9 %all_gather.58 = bf16[384,768]{0,1:T(8,128)(2,1)} all-gather(bf16[384,192]{0,1:T(8,128)(2,1)S(1)} %copy-done.26), channel_id=1, replica_groups=mesh['rows'=8,'head'=4] {'head'}, dimensions={1}, use_global_device_ids=true | all-gather | bytes 737280 | tf_op jit(solution)/shard_map/all_gather | solution.py:125
  131.9 18.8 %all-gather.4 = bf16[8,96,4]{1,2,0:T(4,128)(2,1)S(1)} all-gather(bf16[1,96,4]{1,2,0:T(4,128)(2,1)S(1)} %bitcast.452), channel_id=1, replica_groups=mesh['rows'=8,'head'=4] {'rows'}, dimensions={0}, use_global_device_ids=true | all-gather | bytes 6912 | tf_op jit(solution)/shard_map/all_gather | solution.py:135
  168.7 23.9 %while.45 = (s32[]{:T(128)}, bf16[4,512,3,64]{1,3,2,0:T(8,128)(2,1)}, f32[4,3,512]{2,1,0:T(4,128)S(1)}, bf16[4,512,3,64]{1,3,2,0:T(8,128)(2,1)S(1)}, s32[4]{0:T(...) while((s32[]{:T(128)}, ...), condition=%wide.region_11.12_spmd, body=%wide.region_8.11_spmd.sunk | while | flops 211385856 | bytes 11335809 | solution.py:188
  202.6 27.6 %while.44 = (s32[]{:T(128)}, bf16[4,512,3,64]{1,3,2,0:T(8,128)(2,1)}, f32[4,3,512]{2,1,0:T(4,128)S(1)}, bf16[4,512,3,64]{1,3,2,0:T(8,128)(2,1)}, s32[4]{0:T(128)...) while((s32[]{:T(128)}, ...), condition=%wide.region_3.4_spmd, body=%wide.region_0.3_spmd.sunk | while | flops 211385856 | bytes 11331713 | solution.py:188
  237.5 8.6 all-to-all-done.1
  257.4 31.4 %fusion.100 = (bf16[512,3072]{1,0:T(8,128)(2,1)}, bf16[512,3072]{1,0:T(8,128)(2,1)}, f32[512,3072]{1,0:T(8,128)}) fusion(f32[3072]{0:T(1024)S(1)} %add.262, f32[512,3072]{1,0:T(8,128)S(1)} %fusion.187, bf16[768,3072]{1,0:T(8,128)(2,1)S(1)} %copy-done.45, f32[512,768]{1,0:T(8,128)S(1)} %copy-done.20, f32[768]{0:T(1024)S(1)} %get-tuple-element.270, ...), kind=kOutput, calls=%fused_computation.133 | convolution fusion | flops 2625503232 | bytes 25188352 | tf_op jit(solution)/shard_map/dot_general | solution.py:197
  303.9 8.4 fusion.202
  359.3 37.8 %while.46 = (s32[]{:T(128)}, bf16[4,512,3,3,64]{1,4,3,2,0:T(8,128)(2,1)}, bf16[4,512,3,64]{1,3,2,0:T(8,128)(2,1)S(1)}, s32[4]{0:T(128)S(1)}, s32[4]{0:T(128)S(1)...) while((s32[]{:T(128)}, ...), condition=%wide.region_22.23_spmd, body=%wide.region_20.22_spmd.sunk | while | flops 511999488 | bytes 27300500 | solution.py:224
  403.5 42.0 %while.47 = (s32[]{:T(128)}, bf16[4,512,3,3,64]{1,4,3,2,0:T(8,128)(2,1)}, bf16[4,512,3,64]{1,3,2,0:T(8,128)(2,1)S(1)}, s32[4]{0:T(128)S(1)}, s32[4]{0:T(128)S(1)...) while((s32[]{:T(128)}, ...), condition=%wide.region_29.30_spmd, body=%wide.region_27.29_spmd.sunk | while | flops 511999488 | bytes 30446764 | solution.py:224
  457.4 21.6 %all-to-all-done.7 = bf16[4,512,1,576]{1,3,2,0:T(8,128)(2,1)S(1)} async-done(((bf16[4,512,1,576]{1,3,2,0:T(8,128)(2,1)}), bf16[4,512,1,576]{1,3,2,0:T(8,128)(2,1)S(1)}, u32[]{:S(2)}, u32[]{:S(2)}) %all-to-all-start.7) | async-done | bytes 2359328 | tf_op jit(solution)/shard_map/all_to_all | solution.py:114
  508.9 8.9 fusion.151
  517.9 11.8 convolution_add_fusion.1
  536.8 83.9 %reduce-scatter.31.cloned.1.call-done = f32[96,2304]{1,0:T(8,128)} async-done(((f32[768,2304]{1,0:T(8,128)}), f32[96,2304]{1,0:T(8,128)}) %reduce-scatter.31.cloned.1.call-update) | async-done | bytes 884752
  623.0 162.5 %reduce-scatter.29.cloned.1.call-done = f32[384,768]{1,0:T(8,128)} async-done(((f32[3072,768]{1,0:T(8,128)}), f32[384,768]{1,0:T(8,128)}) %reduce-scatter.29.cloned.1.call-update) | async-done | bytes 1179664 | tf_op jit(solution)/shard_map/reduce_scatter | solution.py:144
  793.9 56.8 %reduce-scatter.39.cloned.1.call-done = f32[96,4]{1,0:T(8,128)} async-done(((f32[768,4]{1,0:T(8,128)}), f32[96,4]{1,0:T(8,128)}) %reduce-scatter.39.cloned.1.call-update) | async-done | bytes 1552
  851.6 163.9 %reduce-scatter.25.cloned.1.call-done = f32[96,3072]{1,0:T(8,128)} async-done(((f32[768,3072]{1,0:T(8,128)}), f32[96,3072]{1,0:T(8,128)}) %reduce-scatter.25.cloned.1.call-update) | async-done | bytes 1179664 | tf_op jit(solution)/shard_map/reduce_scatter | solution.py:143
  1027.0 53.0 %reduce-scatter.37.cloned.1.call-done = f32[96,8]{1,0:T(8,128)} async-done(((f32[768,8]{1,0:T(8,128)}), f32[96,8]{1,0:T(8,128)}) %reduce-scatter.37.cloned.1.call-update) | async-done | bytes 3088
  1088.2 13.6 %reduce-scatter.33.cloned.1.call-done = bf16[192,96]{1,0:T(8,128)(2,1)} async-done(((bf16[768,96]{1,0:T(8,128)(2,1)}), bf16[192,96]{1,0:T(8,128)(2,1)}) %reduce-scatter.33.cloned.1.call-update) | async-done | bytes 36880
  1103.4 22.9 %reduce-scatter.21.cloned.1.call-done = bf16[96,576]{0,1:T(8,128)(2,1)} async-done(((bf16[96,2304]{0,1:T(8,128)(2,1)}), bf16[96,576]{0,1:T(8,128)(2,1)}) %reduce-scatter.21.cloned.1.call-update) | async-done | bytes 110608 | tf_op jit(solution)/shard_map/reduce_scatter | solution.py:149
  1128.0 22.8 %reduce-scatter.35.cloned.1.call-done = bf16[192,384]{1,0:T(8,128)(2,1)} async-done(((bf16[768,384]{1,0:T(8,128)(2,1)}), bf16[192,384]{1,0:T(8,128)(2,1)}) %reduce-scatter.35.cloned.1.call-update) | async-done | bytes 147472
  1152.7 22.5 %reduce-scatter.27.cloned.1.call-done = bf16[96,768]{1,0:T(8,128)(2,1)} async-done(((bf16[96,3072]{1,0:T(8,128)(2,1)}), bf16[96,768]{1,0:T(8,128)(2,1)}) %reduce-scatter.27.cloned.1.call-update) | async-done | bytes 147472 | tf_op jit(solution)/shard_map/reduce_scatter | solution.py:155
  (457 shorter events, 369.8 us)
Async XLA Ops:
  7.2 76.1 %all-gather.10.cloned.1.call-start = ((), (), s32[]{:S(2)}) async-start(), calls=%async_computation.18 | async-start | bytes 3981312 | tf_op jit(solution)/shard_map/all_gather | solution.py:130
  17.5 216.9 %all-gather.12.cloned.1.call-start = ((), (), s32[]{:S(2)}) async-start(), calls=%async_computation.19 | async-start | bytes 1327104 | tf_op jit(solution)/shard_map/all_gather | solution.py:131
  24.9 225.0 %all-gather.14.cloned.1.call-start = ((), (), s32[]{:S(2)}) async-start(), calls=%async_computation.20 | async-start | bytes 5308416 | tf_op jit(solution)/shard_map/all_gather | solution.py:132
  90.0 71.3 %all-to-all-start.2 = ((bf16[1,512,4,576]{1,3,0,2:T(8,128)(2,1)}), bf16[1,512,4,576]{1,3,0,2:T(8,128)(2,1)S(1)}, u32[]{:S(2)}, u32[]{:S(2)}) async-start(bf16[1,512,4,576]{1,3,0,2:T(8,128)(2,1)} %bitcast.436), calls=%async_computation.2 | async-start | bytes 4718592 | tf_op jit(solution)/shard_map/all_to_all | solution.py:93
  93.8 195.0 %all-gather.16.cloned.1.call-start = ((), (), s32[]{:S(2)}) async-start(), calls=%async_computation.21 | async-start | bytes 5308416 | tf_op jit(solution)/shard_map/all_gather | solution.py:133
  161.4 33.1 %all-to-all-start = ((bf16[1,512,4,576]{1,3,0,2:T(8,128)(2,1)}), bf16[1,512,4,576]{1,3,0,2:T(8,128)(2,1)}, u32[]{:S(2)}, u32[]{:S(2)}) async-start(bf16[1,512,4,576]{1,3,0,2:T(8,128)(2,1)} %bitcast.52), calls=%async_computation | async-start | bytes 4718592 | tf_op jit(solution)/shard_map/all_to_all | solution.py:93
  194.5 35.7 %all-to-all-start.3 = ((bf16[4,512,1,192]{1,3,2,0:T(8,128)(2,1)}), bf16[4,512,1,192]{1,3,2,0:T(8,128)(2,1)}, u32[]{:S(2)}, u32[]{:S(2)}) async-start(bf16[4,512,1,192]{1,3,2,0:T(8,128)(2,1)} %bitcast.85), calls=%async_computation.3 | async-start | bytes 1572864 | tf_op jit(solution)/shard_map/all_to_all | solution.py:99
  230.2 15.9 %all-to-all-start.1 = ((bf16[4,512,1,192]{1,3,2,0:T(8,128)(2,1)}), bf16[4,512,1,192]{1,3,2,0:T(8,128)(2,1)}, u32[]{:S(2)}, u32[]{:S(2)}) async-start(bf16[4,512,1,192]{1,3,2,0:T(8,128)(2,1)} %bitcast.63), calls=%async_computation.1 | async-start | bytes 1572864 | tf_op jit(solution)/shard_map/all_to_all | solution.py:99
  339.0 15.1 %all-to-all-start.4 = ((bf16[1,512,4,192]{1,3,0,2:T(8,128)(2,1)}), bf16[1,512,4,192]{1,3,0,2:T(8,128)(2,1)S(1)}, u32[]{:S(2)}, u32[]{:S(2)}) async-start(bf16[1,512,4,192]{1,3,0,2:T(8,128)(2,1)} %bitcast.92), calls=%async_computation.4 | async-start | bytes 1572864 | tf_op jit(solution)/shard_map/all_to_all | solution.py:108
  342.5 192.4 %reduce-scatter.23.cloned.1.call-start = ((), (), s32[]{:S(2)}) async-start(), calls=%async_computation.23 | async-start | bytes 2654208 | tf_op jit(solution)/shard_map/reduce_scatter | solution.py:142
  354.1 43.0 %all-to-all-start.6 = ((bf16[1,512,4,192]{1,3,0,2:T(8,128)(2,1)}), bf16[1,512,4,192]{1,3,0,2:T(8,128)(2,1)S(1)}, u32[]{:S(2)}, u32[]{:S(2)}) async-start(bf16[1,512,4,192]{1,3,0,2:T(8,128)(2,1)} %bitcast.437), calls=%async_computation.6 | async-start | bytes 1572864 | tf_op jit(solution)/shard_map/all_to_all | solution.py:108
  397.9 47.6 %all-to-all-start.5 = ((bf16[4,512,1,576]{1,3,2,0:T(8,128)(2,1)}), bf16[4,512,1,576]{1,3,2,0:T(8,128)(2,1)S(1)}, u32[]{:S(2)}, u32[]{:S(2)}) async-start(bf16[4,512,1,576]{1,3,2,0:T(8,128)(2,1)} %bitcast.97), calls=%async_computation.5 | async-start | bytes 4718592 | tf_op jit(solution)/shard_map/all_to_all | solution.py:114
  446.9 32.1 %all-to-all-start.7 = ((bf16[4,512,1,576]{1,3,2,0:T(8,128)(2,1)}), bf16[4,512,1,576]{1,3,2,0:T(8,128)(2,1)S(1)}, u32[]{:S(2)}, u32[]{:S(2)}) async-start(bf16[4,512,1,576]{1,3,2,0:T(8,128)(2,1)} %bitcast.109), calls=%async_computation.7 | async-start | bytes 4718592 | tf_op jit(solution)/shard_map/all_to_all | solution.py:114
  450.6 170.1 %reduce-scatter.31.cloned.1.call-start = ((), (), s32[]{:S(2)}) async-start(), calls=%async_computation.27 | async-start | bytes 7962624
  495.2 290.3 %reduce-scatter.29.cloned.1.call-start = ((), (), s32[]{:S(2)}) async-start(), calls=%async_computation.26 | async-start | bytes 10616832 | tf_op jit(solution)/shard_map/reduce_scatter | solution.py:144
  506.2 344.5 %reduce-scatter.39.cloned.1.call-start = ((), (), s32[]{:S(2)}) async-start(), calls=%async_computation.31 | async-start | bytes 442368
  517.9 497.6 %reduce-scatter.25.cloned.1.call-start = ((), (), s32[]{:S(2)}) async-start(), calls=%async_computation.24 | async-start | bytes 10616832 | tf_op jit(solution)/shard_map/reduce_scatter | solution.py:143
  529.7 550.3 %reduce-scatter.37.cloned.1.call-start = ((), (), s32[]{:S(2)}) async-start(), calls=%async_computation.30 | async-start | bytes 442368
  534.8 567.1 %reduce-scatter.33.cloned.1.call-start = ((), (), s32[]{:S(2)}) async-start(), calls=%async_computation.28 | async-start | bytes 245760
  535.9 254.3 %copy-start.49 = (u32[32]{0:T(128)S(1)}, u32[32]{0:T(128)}, u32[]{:S(2)}) copy-start(u32[32]{0:T(128)} %constant.177) | copy-start | bytes 388
  535.9 255.6 %copy-start.19 = (bf16[1,1,512,768]{3,2,1,0:T(8,128)(2,1)S(1)}, bf16[1,1,512,768]{3,2,1,0:T(8,128)(2,1)}, u32[]{:S(2)}) copy-start(bf16[1,1,512,768]{3,2,1,0:T(8,128)(2,1)} %get-tuple-element.373) | copy-start | bytes 2359300
  536.7 589.6 %reduce-scatter.21.cloned.1.call-start = ((), (), s32[]{:S(2)}) async-start(), calls=%async_computation.22 | async-start | bytes 737280 | tf_op jit(solution)/shard_map/reduce_scatter | solution.py:149
  623.0 527.9 %reduce-scatter.35.cloned.1.call-start = ((), (), s32[]{:S(2)}) async-start(), calls=%async_computation.29 | async-start | bytes 737280
  789.9 385.4 %reduce-scatter.27.cloned.1.call-start = ((), (), s32[]{:S(2)}) async-start(), calls=%async_computation.25 | async-start | bytes 737280 | tf_op jit(solution)/shard_map/reduce_scatter | solution.py:155
  (57 other events, 736.2 us)
Sparse Core Ops, SparseCore 0:
  17.6 65.6 all-gather.9
  86.1 39.7 all-gather.11
  128.1 78.0 all-gather.13
  208.1 78.9 all-gather.15
  348.6 67.5 reduce-scatter.22
  495.3 125.2 reduce-scatter.30
  624.3 161.2 reduce-scatter.28
  789.4 61.2 reduce-scatter.38
  854.3 161.1 reduce-scatter.24
  1018.6 61.3 reduce-scatter.36
  1083.0 18.7 reduce-scatter.32
  1104.2 22.0 reduce-scatter.20
  1128.8 22.0 reduce-scatter.34
  1153.2 22.0 reduce-scatter.26
where the time goes:
time: 1190 us; the launch traced here: 1180 us
  waiting for transfers between devices  657 us (55%)
  matrix products  213 us (18%)
  blocking collectives  117 us (10%)
  local copies, waits for them, and re-layouts  79.6 us (7%)
  other arithmetic  68.8 us (6%)
  starting transfers between devices  32.3 us (3%)
  between operations  16 us (1%)
    unnamed x19, waiting for transfers between devices  230 us
    reduce_scatter x1, waiting for transfers between devices, reduce_grads(): lax.psum_scatter(running[2], 'rows', scatter_dimension=0, tiled=True)  164 us
    reduce_scatter x1, waiting for transfers between devices, reduce_grads(): lax.psum_scatter(running[3], 'rows', scatter_dimension=0, tiled=True)  163 us
    dot_general x8, matrix products, contract_rows(): lax.dot_general(left, right, (((0,), (0,)), ((), ())), preferred_element_...  52.4 us
    dot_general x2, matrix products, layer_step(): jnp.dot(hidden_low, up_full, preferred_element_type=jnp.float32)  36.3 us
    dot_general x8, matrix products, contract_cols(): lax.dot_general(left, right, (((1,), (1,)), ((), ())), preferred_element_...  36.1 us
    all_gather x1, blocking collectives, gather_weights(): lax.all_gather(down_weight, 'head', axis=1, tiled=True)  32.9 us
    unnamed x126, local copies, waits for them, and re-layouts  30.5 us
  transfers between devices with their start and end apart: 22, of which 14 were waited for; matrix products, arithmetic and copies ran while one was open for 26% of the time, Pallas kernels for 0%

commit v1 on v0

--- a/solution.py
+++ b/solution.py
@@ -111,8 +111,16 @@
 
 def grad_to_tokens(grad_items, seq_per):
     width = grad_items.shape[2] * 3 * HD
-    joined = lax.all_to_all(
-        grad_items.reshape(-1, SEQ, 1, width), "head", split_axis=0, concat_axis=2, tiled=True
+    joined = jnp.concatenate(
+        lax.all_to_all(
+            jnp.stack(
+                jnp.split(grad_items.reshape(-1, SEQ, 1, width), lax.axis_size("head"), 0), 0
+            ),
+            "head",
+            split_axis=0,
+            concat_axis=0,
+        ),
+        2,
     )
     return joined.reshape(seq_per * SEQ, 3 * D)
 

time: 1190 us -> 1200 us (level)
    unnamed x126 -> x128, local copies, waits for them, and re-layouts: 30.5 us -> 30.6 us
where the time goes in v1:
time: 1200 us; the launch traced here: 1190 us
  waiting for transfers between devices  657 us (55%)
  matrix products  213 us (18%)
  blocking collectives  117 us (10%)
  local copies, waits for them, and re-layouts  83.1 us (7%)
  other arithmetic  72.2 us (6%)
  starting transfers between devices  32.3 us (3%)
  between operations  16 us (1%)
    unnamed x19, waiting for transfers between devices  230 us
    reduce_scatter x1, waiting for transfers between devices, reduce_grads(): lax.psum_scatter(running[2], 'rows', scatter_dimension=0, tiled=True)  164 us
    reduce_scatter x1, waiting for transfers between devices, reduce_grads(): lax.psum_scatter(running[3], 'rows', scatter_dimension=0, tiled=True)  163 us
    dot_general x8, matrix products, contract_rows(): lax.dot_general(left, right, (((0,), (0,)), ((), ())), preferred_element_...  52.4 us
    dot_general x8, matrix products, contract_cols(): lax.dot_general(left, right, (((1,), (1,)), ((), ())), preferred_element_...  36.7 us
    dot_general x2, matrix products, layer_step(): jnp.dot(hidden_low, up_full, preferred_element_type=jnp.float32)  36.3 us
    all_gather x1, blocking collectives, gather_weights(): lax.all_gather(down_weight, 'head', axis=1, tiled=True)  32.9 us
    unnamed x128, local copies, waits for them, and re-layouts  30.6 us
  transfers between devices with their start and end apart: 22, of which 14 were waited for; matrix products, arithmetic and copies ran while one was open for 26% of the time, Pallas kernels for 0%

profile of v1, /device:TPU:0, one launch (start us, length us, event | category | flops | bytes accessed | tf_op | source)
XLA Modules:
  0.0 1191.1 jit_solution(2883270533605068719)
XLA Ops:
  7.2 8.8 all-gather
  38.1 27.4 %all-gather.2 = bf16[8,96,8]{1,2,0:T(8,128)(2,1)S(1)} all-gather(bf16[1,96,8]{1,2,0:T(8,128)(2,1)S(1)} %bitcast.457), channel_id=1, replica_groups=mesh['rows'=8,'head'=4] {'rows'}, dimensions={0}, use_global_device_ids=true | all-gather | bytes 13824 | tf_op jit(solution)/shard_map/all_gather | solution.py:142
  66.6 16.7 %all-gather.10.cloned.1.call-done = bf16[768,2304]{1,0:T(8,128)(2,1)} async-done(((bf16[96,2304]{1,0:T(8,128)(2,1)}), bf16[768,2304]{1,0:T(8,128)(2,1)}) %all-gather.10.cloned.1.call-update) | async-done | bytes 3538960 | tf_op jit(solution)/shard_map/all_gather | solution.py:138
  93.9 32.9 %all_gather.58 = bf16[384,768]{0,1:T(8,128)(2,1)} all-gather(bf16[384,192]{0,1:T(8,128)(2,1)S(1)} %copy-done.26), channel_id=1, replica_groups=mesh['rows'=8,'head'=4] {'head'}, dimensions={1}, use_global_device_ids=true | all-gather | bytes 737280 | tf_op jit(solution)/shard_map/all_gather | solution.py:133
  131.9 18.8 %all-gather.4 = bf16[8,96,4]{1,2,0:T(4,128)(2,1)S(1)} all-gather(bf16[1,96,4]{1,2,0:T(4,128)(2,1)S(1)} %bitcast.458), channel_id=1, replica_groups=mesh['rows'=8,'head'=4] {'rows'}, dimensions={0}, use_global_device_ids=true | all-gather | bytes 6912 | tf_op jit(solution)/shard_map/all_gather | solution.py:143
  168.7 23.9 %while.45 = (s32[]{:T(128)}, bf16[4,512,3,64]{1,3,2,0:T(8,128)(2,1)}, f32[4,3,512]{2,1,0:T(4,128)S(1)}, bf16[4,512,3,64]{1,3,2,0:T(8,128)(2,1)S(1)}, s32[4]{0:T(...) while((s32[]{:T(128)}, ...), condition=%wide.region_11.12_spmd, body=%wide.region_8.11_spmd.sunk | while | flops 211385856 | bytes 11335809 | solution.py:196
  202.6 27.6 %while.44 = (s32[]{:T(128)}, bf16[4,512,3,64]{1,3,2,0:T(8,128)(2,1)}, f32[4,3,512]{2,1,0:T(4,128)S(1)}, bf16[4,512,3,64]{1,3,2,0:T(8,128)(2,1)}, s32[4]{0:T(128)...) while((s32[]{:T(128)}, ...), condition=%wide.region_3.4_spmd, body=%wide.region_0.3_spmd.sunk | while | flops 211385856 | bytes 11331713 | solution.py:196
  237.5 8.6 all-to-all-done.1
  257.4 31.4 %fusion.100 = (bf16[512,3072]{1,0:T(8,128)(2,1)}, bf16[512,3072]{1,0:T(8,128)(2,1)}, f32[512,3072]{1,0:T(8,128)}) fusion(f32[3072]{0:T(1024)S(1)} %add.262, f32[512,3072]{1,0:T(8,128)S(1)} %fusion.187, bf16[768,3072]{1,0:T(8,128)(2,1)S(1)} %copy-done.46, f32[512,768]{1,0:T(8,128)S(1)} %copy-done.20, f32[768]{0:T(1024)S(1)} %get-tuple-element.270, ...), kind=kOutput, calls=%fused_computation.133 | convolution fusion | flops 2625503232 | bytes 25188352 | tf_op jit(solution)/shard_map/dot_general | solution.py:205
  303.9 8.4 fusion.204
  359.8 37.8 %while.46 = (s32[]{:T(128)}, bf16[4,512,3,3,64]{1,4,3,2,0:T(8,128)(2,1)}, bf16[4,512,3,64]{1,3,2,0:T(8,128)(2,1)S(1)}, s32[4]{0:T(128)S(1)}, s32[4]{0:T(128)S(1)...) while((s32[]{:T(128)}, ...), condition=%wide.region_22.23_spmd, body=%wide.region_20.22_spmd.sunk | while | flops 511999488 | bytes 27300500 | solution.py:232
  407.5 41.8 %while.47 = (s32[]{:T(128)}, bf16[4,512,3,3,64]{1,4,3,2,0:T(8,128)(2,1)}, bf16[4,512,3,64]{1,3,2,0:T(8,128)(2,1)S(1)}, s32[4]{0:T(128)S(1)}, s32[4]{0:T(128)S(1)...) while((s32[]{:T(128)}, ...), condition=%wide.region_29.30_spmd, body=%wide.region_27.29_spmd.sunk | while | flops 511999488 | bytes 30446764 | solution.py:232
  464.7 21.6 %all-to-all-done.7 = bf16[4,1,512,1,576]{2,4,3,1,0:T(8,128)(2,1)S(1)} async-done(((bf16[4,1,512,1,576]{2,4,3,1,0:T(8,128)(2,1)}), bf16[4,1,512,1,576]{2,4,3,1,0:T(8,128)(2,1)S(1)}, u32[]{:S(2)}, u32[]{:S(2)}) %all-to-all-start.7) | async-done | bytes 2359328 | tf_op jit(solution)/shard_map/all_to_all | solution.py:115
  516.3 8.9 fusion.151
  525.3 11.8 convolution_add_fusion.1
  544.2 83.8 %reduce-scatter.31.cloned.1.call-done = f32[96,2304]{1,0:T(8,128)} async-done(((f32[768,2304]{1,0:T(8,128)}), f32[96,2304]{1,0:T(8,128)}) %reduce-scatter.31.cloned.1.call-update) | async-done | bytes 884752
  630.3 162.5 %reduce-scatter.29.cloned.1.call-done = f32[384,768]{1,0:T(8,128)} async-done(((f32[3072,768]{1,0:T(8,128)}), f32[384,768]{1,0:T(8,128)}) %reduce-scatter.29.cloned.1.call-update) | async-done | bytes 1179664 | tf_op jit(solution)/shard_map/reduce_scatter | solution.py:152
  801.2 56.8 %reduce-scatter.39.cloned.1.call-done = f32[96,4]{1,0:T(8,128)} async-done(((f32[768,4]{1,0:T(8,128)}), f32[96,4]{1,0:T(8,128)}) %reduce-scatter.39.cloned.1.call-update) | async-done | bytes 1552
  858.9 163.9 %reduce-scatter.25.cloned.1.call-done = f32[96,3072]{1,0:T(8,128)} async-done(((f32[768,3072]{1,0:T(8,128)}), f32[96,3072]{1,0:T(8,128)}) %reduce-scatter.25.cloned.1.call-update) | async-done | bytes 1179664 | tf_op jit(solution)/shard_map/reduce_scatter | solution.py:151
  1034.3 52.9 %reduce-scatter.37.cloned.1.call-done = f32[96,8]{1,0:T(8,128)} async-done(((f32[768,8]{1,0:T(8,128)}), f32[96,8]{1,0:T(8,128)}) %reduce-scatter.37.cloned.1.call-update) | async-done | bytes 3088
  1095.4 13.6 %reduce-scatter.33.cloned.1.call-done = bf16[192,96]{1,0:T(8,128)(2,1)} async-done(((bf16[768,96]{1,0:T(8,128)(2,1)}), bf16[192,96]{1,0:T(8,128)(2,1)}) %reduce-scatter.33.cloned.1.call-update) | async-done | bytes 36880
  1110.6 22.9 %reduce-scatter.21.cloned.1.call-done = bf16[96,576]{0,1:T(8,128)(2,1)} async-done(((bf16[96,2304]{0,1:T(8,128)(2,1)}), bf16[96,576]{0,1:T(8,128)(2,1)}) %reduce-scatter.21.cloned.1.call-update) | async-done | bytes 110608 | tf_op jit(solution)/shard_map/reduce_scatter | solution.py:157
  1135.2 22.8 %reduce-scatter.35.cloned.1.call-done = bf16[192,384]{1,0:T(8,128)(2,1)} async-done(((bf16[768,384]{1,0:T(8,128)(2,1)}), bf16[192,384]{1,0:T(8,128)(2,1)}) %reduce-scatter.35.cloned.1.call-update) | async-done | bytes 147472
  1159.9 22.5 %reduce-scatter.27.cloned.1.call-done = bf16[96,768]{1,0:T(8,128)(2,1)} async-done(((bf16[96,3072]{1,0:T(8,128)(2,1)}), bf16[96,768]{1,0:T(8,128)(2,1)}) %reduce-scatter.27.cloned.1.call-update) | async-done | bytes 147472 | tf_op jit(solution)/shard_map/reduce_scatter | solution.py:163
  (463 shorter events, 377.2 us)
Async XLA Ops:
  7.2 76.1 %all-gather.10.cloned.1.call-start = ((), (), s32[]{:S(2)}) async-start(), calls=%async_computation.18 | async-start | bytes 3981312 | tf_op jit(solution)/shard_map/all_gather | solution.py:138
  17.5 216.9 %all-gather.12.cloned.1.call-start = ((), (), s32[]{:S(2)}) async-start(), calls=%async_computation.19 | async-start | bytes 1327104 | tf_op jit(solution)/shard_map/all_gather | solution.py:139
  24.9 225.0 %all-gather.14.cloned.1.call-start = ((), (), s32[]{:S(2)}) async-start(), calls=%async_computation.20 | async-start | bytes 5308416 | tf_op jit(solution)/shard_map/all_gather | solution.py:140
  90.0 71.3 %all-to-all-start.2 = ((bf16[1,512,4,576]{1,3,0,2:T(8,128)(2,1)}), bf16[1,512,4,576]{1,3,0,2:T(8,128)(2,1)S(1)}, u32[]{:S(2)}, u32[]{:S(2)}) async-start(bf16[1,512,4,576]{1,3,0,2:T(8,128)(2,1)} %bitcast.434), calls=%async_computation.2 | async-start | bytes 4718592 | tf_op jit(solution)/shard_map/all_to_all | solution.py:93
  93.8 195.1 %all-gather.16.cloned.1.call-start = ((), (), s32[]{:S(2)}) async-start(), calls=%async_computation.21 | async-start | bytes 5308416 | tf_op jit(solution)/shard_map/all_gather | solution.py:141
  161.4 33.1 %all-to-all-start = ((bf16[1,512,4,576]{1,3,0,2:T(8,128)(2,1)}), bf16[1,512,4,576]{1,3,0,2:T(8,128)(2,1)}, u32[]{:S(2)}, u32[]{:S(2)}) async-start(bf16[1,512,4,576]{1,3,0,2:T(8,128)(2,1)} %bitcast.52), calls=%async_computation | async-start | bytes 4718592 | tf_op jit(solution)/shard_map/all_to_all | solution.py:93
  194.5 35.7 %all-to-all-start.3 = ((bf16[4,512,1,192]{1,3,2,0:T(8,128)(2,1)}), bf16[4,512,1,192]{1,3,2,0:T(8,128)(2,1)}, u32[]{:S(2)}, u32[]{:S(2)}) async-start(bf16[4,512,1,192]{1,3,2,0:T(8,128)(2,1)} %bitcast.85), calls=%async_computation.3 | async-start | bytes 1572864 | tf_op jit(solution)/shard_map/all_to_all | solution.py:99
  230.2 15.9 %all-to-all-start.1 = ((bf16[4,512,1,192]{1,3,2,0:T(8,128)(2,1)}), bf16[4,512,1,192]{1,3,2,0:T(8,128)(2,1)}, u32[]{:S(2)}, u32[]{:S(2)}) async-start(bf16[4,512,1,192]{1,3,2,0:T(8,128)(2,1)} %bitcast.63), calls=%async_computation.1 | async-start | bytes 1572864 | tf_op jit(solution)/shard_map/all_to_all | solution.py:99
  339.6 15.1 %all-to-all-start.4 = ((bf16[1,512,4,192]{1,3,0,2:T(8,128)(2,1)}), bf16[1,512,4,192]{1,3,0,2:T(8,128)(2,1)S(1)}, u32[]{:S(2)}, u32[]{:S(2)}) async-start(bf16[1,512,4,192]{1,3,0,2:T(8,128)(2,1)} %bitcast.92), calls=%async_computation.4 | async-start | bytes 1572864 | tf_op jit(solution)/shard_map/all_to_all | solution.py:108
  343.1 199.2 %reduce-scatter.23.cloned.1.call-start = ((), (), s32[]{:S(2)}) async-start(), calls=%async_computation.23 | async-start | bytes 2654208 | tf_op jit(solution)/shard_map/reduce_scatter | solution.py:150
  354.7 46.4 %all-to-all-start.6 = ((bf16[1,512,4,192]{1,3,0,2:T(8,128)(2,1)}), bf16[1,512,4,192]{1,3,0,2:T(8,128)(2,1)S(1)}, u32[]{:S(2)}, u32[]{:S(2)}) async-start(bf16[1,512,4,192]{1,3,0,2:T(8,128)(2,1)} %bitcast.435), calls=%async_computation.6 | async-start | bytes 1572864 | tf_op jit(solution)/shard_map/all_to_all | solution.py:108
  402.0 50.9 %all-to-all-start.5 = ((bf16[4,1,512,1,576]{2,4,3,1,0:T(8,128)(2,1)}), bf16[4,1,512,1,576]{2,4,3,1,0:T(8,128)(2,1)S(1)}, u32[]{:S(2)}, u32[]{:S(2)}) async-start(bf16[4,1,512,1,576]{2,4,3,1,0:T(8,128)(2,1)} %pad_maximum_fusion.3), calls=%async_computation.5 | async-start | bytes 4718592 | tf_op jit(solution)/shard_map/all_to_all | solution.py:115
  454.3 32.1 %all-to-all-start.7 = ((bf16[4,1,512,1,576]{2,4,3,1,0:T(8,128)(2,1)}), bf16[4,1,512,1,576]{2,4,3,1,0:T(8,128)(2,1)S(1)}, u32[]{:S(2)}, u32[]{:S(2)}) async-start(bf16[4,1,512,1,576]{2,4,3,1,0:T(8,128)(2,1)} %pad_maximum_fusion.4), calls=%async_computation.7 | async-start | bytes 4718592 | tf_op jit(solution)/shard_map/all_to_all | solution.py:115
  457.9 170.1 %reduce-scatter.31.cloned.1.call-start = ((), (), s32[]{:S(2)}) async-start(), calls=%async_computation.27 | async-start | bytes 7962624
  502.6 290.3 %reduce-scatter.29.cloned.1.call-start = ((), (), s32[]{:S(2)}) async-start(), calls=%async_computation.26 | async-start | bytes 10616832 | tf_op jit(solution)/shard_map/reduce_scatter | solution.py:152
  513.5 344.5 %reduce-scatter.39.cloned.1.call-start = ((), (), s32[]{:S(2)}) async-start(), calls=%async_computation.31 | async-start | bytes 442368
  525.2 497.6 %reduce-scatter.25.cloned.1.call-start = ((), (), s32[]{:S(2)}) async-start(), calls=%async_computation.24 | async-start | bytes 10616832 | tf_op jit(solution)/shard_map/reduce_scatter | solution.py:151
  537.1 550.1 %reduce-scatter.37.cloned.1.call-start = ((), (), s32[]{:S(2)}) async-start(), calls=%async_computation.30 | async-start | bytes 442368
  542.2 566.9 %reduce-scatter.33.cloned.1.call-start = ((), (), s32[]{:S(2)}) async-start(), calls=%async_computation.28 | async-start | bytes 245760
  543.2 254.3 %copy-start.50 = (u32[32]{0:T(128)S(1)}, u32[32]{0:T(128)}, u32[]{:S(2)}) copy-start(u32[32]{0:T(128)} %constant.177) | copy-start | bytes 388
  543.3 255.5 %copy-start.19 = (bf16[1,1,512,768]{3,2,1,0:T(8,128)(2,1)S(1)}, bf16[1,1,512,768]{3,2,1,0:T(8,128)(2,1)}, u32[]{:S(2)}) copy-start(bf16[1,1,512,768]{3,2,1,0:T(8,128)(2,1)} %get-tuple-element.381) | copy-start | bytes 2359300
  544.1 589.3 %reduce-scatter.21.cloned.1.call-start = ((), (), s32[]{:S(2)}) async-start(), calls=%async_computation.22 | async-start | bytes 737280 | tf_op jit(solution)/shard_map/reduce_scatter | solution.py:157
  630.3 527.8 %reduce-scatter.35.cloned.1.call-start = ((), (), s32[]{:S(2)}) async-start(), calls=%async_computation.29 | async-start | bytes 737280
  797.2 385.3 %reduce-scatter.27.cloned.1.call-start = ((), (), s32[]{:S(2)}) async-start(), calls=%async_computation.25 | async-start | bytes 737280 | tf_op jit(solution)/shard_map/reduce_scatter | solution.py:163
  (58 other events, 738.0 us)
Sparse Core Ops, SparseCore 0:
  17.6 65.6 all-gather.9
  86.1 39.7 all-gather.11
  128.1 78.0 all-gather.13
  208.1 78.9 all-gather.15
  349.2 67.3 reduce-scatter.22
  502.7 125.2 reduce-scatter.30
  631.6 161.2 reduce-scatter.28
  796.7 61.2 reduce-scatter.38
  861.6 161.1 reduce-scatter.24
  1025.9 61.2 reduce-scatter.36
  1090.2 18.7 reduce-scatter.32
  1111.4 22.0 reduce-scatter.20
  1136.0 22.0 reduce-scatter.34
  1160.4 22.0 reduce-scatter.26
